TPU v7x, 32 devices: a whole 2x2x4 slice. The times are simulated.
32 devices in a mesh: seq: 16 (over z, y, x), head: 2 (over core).
Axes of the slice: x: 2, y: 2, z: 4, core: 2. Of those that a mesh axis runs over, the one named last changes fastest.
Arguments:
- queries: bfloat16 [2048, 2048], P('seq', 'head'), may hold values from -6 to 6
- key_vectors: bfloat16 [2, 2048, 2048], P(None, 'seq', 'head'), may hold values from -6 to 6
- values: bfloat16 [2, 2048, 2048], P(None, 'seq', 'head'), may hold values from -6 to 6
- strengths: float32 [2, 16, 2048], P(None, 'head', 'seq'), may hold values from 0.05 to 1.95
- out_weight: bfloat16 [2048, 4096], P('head', 'seq'), may hold values from -0.1875 to 0.1875
Outputs:
- mixed: bfloat16 [2048, 4096], P('seq', 'head')
All inputs are finite; a program needn't handle non-finite values.
Results may differ from a plain program's by a relative error of at most 0.014.
Values may be sent and summed in bfloat16 or wider, within the bound.
No kernel may reach another device: no remote copies, remote signals or barrier semaphores. Data moves between devices by JAX's collectives and lax.ppermute only.
A program may use at most 64 MiB of HBM per device.

v0:
```python
import jax
import jax.numpy as jnp
from jax import lax
from jax.sharding import PartitionSpec as P

BLOCK = 64
HIGHEST_PRECISION = lax.Precision.HIGHEST


def carried_in(value, axis, join, neutral):
    count, mine = (lax.axis_size(axis), lax.axis_index(axis))
    pieces = jax.tree.map(lambda part: lax.all_gather(part, axis), value)
    total = jax.tree.map(
        lambda part, zero: jnp.full_like(part, 0) + jnp.asarray(zero, part.dtype), value, neutral
    )

    def hop(position, total):
        longer = join(total, jax.tree.map(lambda part: part[position], pieces))
        return jax.tree.map(lambda new, old: jnp.where(position < mine, new, old), longer, total)

    return lax.fori_loop(0, count - 1, hop, total)


def unit_rows(matrix):
    return matrix * lax.rsqrt(jnp.sum(matrix * matrix, axis=-1, keepdims=True) + 1e-06)


def block_inputs(inputs, first_row):
    queries, key_vectors, values, strengths = inputs
    head_count = strengths.shape[1]
    head_width = queries.shape[1] // head_count
    query_part = (
        lax.dynamic_slice_in_dim(queries, first_row, BLOCK, 0)
        .astype(jnp.float32)
        .reshape(BLOCK, head_count, head_width)
    )
    key_part = (
        lax.dynamic_slice_in_dim(key_vectors, first_row, BLOCK, 1)
        .astype(jnp.float32)
        .reshape(2, BLOCK, head_count, head_width)
    )
    value_part = (
        lax.dynamic_slice_in_dim(values, first_row, BLOCK, 1)
        .astype(jnp.float32)
        .reshape(2, BLOCK, head_count, head_width)
    )
    beta_part = lax.dynamic_slice_in_dim(strengths, first_row, BLOCK, 2)
    query_heads = jnp.transpose(unit_rows(query_part), (1, 0, 2))
    key_heads = jnp.transpose(unit_rows(key_part), (2, 1, 0, 3)).reshape(
        head_count, 2 * BLOCK, head_width
    )
    value_heads = jnp.transpose(value_part, (2, 1, 0, 3)).reshape(head_count, 2 * BLOCK, head_width)
    beta_heads = jnp.transpose(beta_part, (1, 2, 0)).reshape(head_count, 2 * BLOCK)
    return (query_heads, key_heads, value_heads, beta_heads)


def solve_block(key_heads, right_side, beta_heads):
    key_gram = jnp.einsum("hik,hjk->hij", key_heads, key_heads, precision=HIGHEST_PRECISION)
    system = jnp.tril(key_gram, -1) * beta_heads[:, :, None] + jnp.eye(2 * BLOCK, dtype=jnp.float32)
    return jax.scipy.linalg.solve_triangular(
        system, beta_heads[:, :, None] * right_side, lower=True, unit_diagonal=True
    )


def reach_table():
    row_ids = lax.broadcasted_iota(jnp.int32, (BLOCK, 2 * BLOCK), 0)
    col_ids = lax.broadcasted_iota(jnp.int32, (BLOCK, 2 * BLOCK), 1)
    return (col_ids <= 2 * row_ids + 1).astype(jnp.float32)


def compose(earlier, later):
    product = jnp.einsum("hjk,hkl->hjl", earlier[0], later[0], precision=HIGHEST_PRECISION)
    state = jnp.einsum("hjk,hkl->hjl", earlier[1], later[0], precision=HIGHEST_PRECISION) + later[1]
    return (product, state)


def incoming_state(product, local_state, identity_stack, zero_state):
    prefix = carried_in((product, local_state), "seq", compose, (identity_stack, zero_state))
    return prefix[1]


def per_device(queries, key_vectors, values, strengths, out_weight):
    head_count = strengths.shape[1]
    tok_rows = queries.shape[0]
    head_width = queries.shape[1] // head_count
    inputs = (queries, key_vectors, values, strengths)
    first_rows = jnp.arange(tok_rows // BLOCK, dtype=jnp.int32) * BLOCK
    identity_stack = jnp.broadcast_to(
        jnp.eye(head_width, dtype=jnp.float32), (head_count, head_width, head_width)
    )
    zero_state = jnp.zeros((head_count, head_width, head_width), jnp.float32)
    reach_mask = reach_table()

    def ahead_step(carried, first_row):
        local_state, product = carried
        query_heads, key_heads, value_heads, beta_heads = block_inputs(inputs, first_row)
        solved = solve_block(
            key_heads, jnp.concatenate([key_heads, value_heads], axis=2), beta_heads
        )
        key_weights = solved[:, :, :head_width]
        value_weights = solved[:, :, head_width:]
        scores = (
            jnp.einsum("htk,hik->hti", query_heads, key_heads, precision=HIGHEST_PRECISION)
            * reach_mask
        )
        updates = value_weights - jnp.einsum(
            "hik,hvk->hiv", key_weights, local_state, precision=HIGHEST_PRECISION
        )
        out_local = jnp.einsum(
            "hvk,htk->htv", local_state, query_heads, precision=HIGHEST_PRECISION
        ) + jnp.einsum("hti,hiv->htv", scores, updates, precision=HIGHEST_PRECISION)
        reduced = query_heads - jnp.einsum(
            "hti,hik->htk", scores, key_weights, precision=HIGHEST_PRECISION
        )
        lifted = jnp.einsum("htk,hjk->htj", reduced, product, precision=HIGHEST_PRECISION)
        shrink = identity_stack - jnp.einsum(
            "hik,hil->hkl", key_weights, key_heads, precision=HIGHEST_PRECISION
        )
        local_state = local_state + jnp.einsum(
            "hiv,hik->hvk", updates, key_heads, precision=HIGHEST_PRECISION
        )
        product = jnp.einsum("hjk,hkl->hjl", product, shrink, precision=HIGHEST_PRECISION)
        return ((local_state, product), (out_local, lifted))

    (local_state, product), (out_local, lifted) = lax.scan(
        ahead_step, (zero_state, identity_stack), first_rows
    )
    state_in = incoming_state(product, local_state, identity_stack, zero_state)
    heads_out = out_local + jnp.einsum(
        "nhtk,hvk->nhtv", lifted, state_in, precision=HIGHEST_PRECISION
    )
    mixed_heads = (
        jnp.transpose(heads_out, (0, 2, 1, 3))
        .reshape(tok_rows, head_count * head_width)
        .astype(jnp.bfloat16)
    )
    partial_sums = jnp.dot(
        mixed_heads,
        lax.all_gather(out_weight, "seq", axis=1, tiled=True),
        preferred_element_type=jnp.float32,
    )
    return lax.psum_scatter(
        partial_sums.astype(jnp.bfloat16), "head", scatter_dimension=1, tiled=True
    )


def solution(mesh):
    return jax.shard_map(
        per_device,
        mesh=mesh,
        in_specs=(
            P("seq", "head"),
            P(None, "seq", "head"),
            P(None, "seq", "head"),
            P(None, "head", "seq"),
            P("head", "seq"),
        ),
        out_specs=P("seq", "head"),
        check_vma=False,
    )
```

profile of v0, /device:TPU:0, one launch (start us, length us, event | category | flops | bytes accessed | tf_op | source)
XLA Modules:
  0.0 591.6 jit_solution(15922539583316434189)
XLA Ops:
  6.7 200.9 %while.31 = (s32[]{:T(128)}, f32[8,128,128]{2,1,0:T(8,128)S(1)}, f32[8,128,128]{1,2,0:T(8,128)S(1)}, f32[2,8,64,128]{3,2,0,1:T(8,128)}, f32[2,8,64,128]{3,2,0,1:...) while((s32[]{:T(128)}, f32[8,128,128]{2,1,0:T(8,128)S(1)}, ...), condition=%wide.region_3.4_spmd.clone, body=%wide.region_0.3_spmd.clone.sunk | while | flops 1915912320 | bytes 28152272 | solution.py:125
  13.8 79.2 %custom-call.10 = f32[8,1,128,128]{2,3,1,0:T(8,128)} custom-call(f32[8,1,128,128]{3,2,1,0:T(8,128)S(1)} %fusion.128), custom_call_target="InvertDiagBlocksLowerTriangular" | custom-call | tf_op jit(solution)/shard_map/while/body/eval_jaxpr/jit(_solve_triangular)/vmap()/triangular_solve | solution.py:60
  93.6 2.3 fusion.129
  114.1 79.2 %custom-call.10 = f32[8,1,128,128]{2,3,1,0:T(8,128)} custom-call(f32[8,1,128,128]{3,2,1,0:T(8,128)S(1)} %fusion.128), custom_call_target="InvertDiagBlocksLowerTriangular" | custom-call | tf_op jit(solution)/shard_map/while/body/eval_jaxpr/jit(_solve_triangular)/vmap()/triangular_solve | solution.py:60
  193.9 2.3 fusion.129
  210.3 113.6 %all-gather.8.cloned.1.call-done = f32[128,128,128]{2,1,0:T(8,128)} async-done(((f32[8,128,128]{2,1,0:T(8,128)}), f32[128,128,128]{2,1,0:T(8,128)}) %all-gather.8.cloned.1.call-update) | async-done | bytes 8388624 | tf_op jit(solution)/shard_map/all_gather | solution.py:12
  323.9 113.3 %all-gather.10.cloned.1.call-done = f32[128,128,128]{2,1,0:T(8,128)} async-done(((f32[8,128,128]{2,1,0:T(8,128)}), f32[128,128,128]{2,1,0:T(8,128)}) %all-gather.10.cloned.1.call-update) | async-done | bytes 8388624 | tf_op jit(solution)/shard_map/all_gather | solution.py:12
  437.2 51.5 %while.32 = (s32[]{:T(128)}, f32[8,128,128]{1,2,0:T(8,128)S(1)}, s32[]{:T(128)}, f32[16,8,128,128]{3,2,1,0:T(8,128)}, f32[16,8,128,128]{3,2,1,0:T(8,128)}, /*index=5*/s32[]{:T(128)}, s32[]{:T(128)}) while((s32[]{:T(128)}, f32[8,128,128]{1,2,0:T(8,128)S(1)}, s32[]{:T(128)}, f32[16,8,128,128]{3,2,1,0:T(8,128)}, ...), condition=%wide.region_5.6_spmd.clone, body=%wide.region_4.5_spmd.clone.sunk | while | flops 201850880 | bytes 5769315 | solution.py:21
  438.6 2.1 fusion.136
  442.0 2.1 fusion.136
  445.4 2.1 fusion.136
  448.9 2.1 fusion.136
  452.3 2.1 fusion.136
  455.8 2.1 fusion.136
  459.2 2.1 fusion.136
  462.6 2.1 fusion.136
  466.0 2.1 fusion.136
  469.4 2.1 fusion.136
  472.9 2.1 fusion.136
  483.2 2.1 fusion.136
  486.6 2.1 fusion.136
  489.5 83.1 %all-gather.6.cloned.1.call-done = bf16[1024,4096]{1,0:T(8,128)(2,1)} async-done(((bf16[1024,256]{1,0:T(8,128)(2,1)}), bf16[1024,4096]{1,0:T(8,128)(2,1)}) %all-gather.6.cloned.1.call-update) | async-done | bytes 8388624 | tf_op jit(solution)/shard_map/all_gather | solution.py:139
  572.6 5.7 convolution_convert_fusion
  578.3 6.7 %reduce-scatter.2.cloned.1.call-done = bf16[128,2048]{1,0:T(8,128)(2,1)} async-done(((bf16[128,4096]{1,0:T(8,128)(2,1)}), bf16[128,2048]{1,0:T(8,128)(2,1)}) %reduce-scatter.2.cloned.1.call-update) | async-done | bytes 524304 | tf_op jit(solution)/shard_map/reduce_scatter | solution.py:142
  (139 shorter events, 61.0 us)
Async XLA Ops:
  6.5 317.4 %all-gather.8.cloned.1.call-start = ((), (), s32[]{:S(2)}) async-start(), calls=%async_computation.3 | async-start | bytes 8912896 | tf_op jit(solution)/shard_map/all_gather | solution.py:12
  207.6 1.1 copy-start
  208.7 228.5 %all-gather.10.cloned.1.call-start = ((), (), s32[]{:S(2)}) async-start(), calls=%async_computation.4 | async-start | bytes 8912896 | tf_op jit(solution)/shard_map/all_gather | solution.py:12
  209.5 363.1 %all-gather.6.cloned.1.call-start = ((), (), s32[]{:S(2)}) async-start(), calls=%async_computation.1 | async-start | bytes 8912896 | tf_op jit(solution)/shard_map/all_gather | solution.py:139
  210.2 374.8 %reduce-scatter.2.cloned.1.call-start = ((), (), s32[]{:S(2)}) async-start(), calls=%async_computation.2 | async-start | bytes 1572864 | tf_op jit(solution)/shard_map/reduce_scatter | solution.py:142
  437.2 51.5 %copy-start.1 = (f32[2,8,64,128]{3,2,0,1:T(8,128)S(1)}, f32[2,8,64,128]{3,2,0,1:T(8,128)}, u32[]{:S(2)}) copy-start(f32[2,8,64,128]{3,2,0,1:T(8,128)} %get-tuple-element.164) | copy-start | bytes 1572868
  437.2 51.5 %copy-start.2 = (f32[2,8,64,128]{3,2,0,1:T(8,128)S(1)}, f32[2,8,64,128]{3,2,0,1:T(8,128)}, u32[]{:S(2)}) copy-start(f32[2,8,64,128]{3,2,0,1:T(8,128)} %get-tuple-element.168) | copy-start | bytes 1572868
Sparse Core Ops, SparseCore 0:
  208.8 115.0 all-gather.7
  326.7 110.4 all-gather.9
  439.9 132.6 all-gather.5
  578.4 6.5 reduce-scatter.1
where the time goes:
time: 593 us; the launch traced here: 592 us
  waiting for transfers between devices  318 us (54%)
  other arithmetic  164 us (28%)
  matrix products  64 us (11%)
  local copies, waits for them, and re-layouts  26.7 us (5%)
  between operations  13.3 us (2%)
    all_gather x2, waiting for transfers between devices, carried_in(): pieces = jax.tree.map(lambda part: lax.all_gather(part, axis), value)  227 us
    another operation x8, other arithmetic, solve_block(): jax.scipy.linalg.solve_triangular(system, beta_heads[:, :, None] * right_...  159 us
    all_gather x1, waiting for transfers between devices, per_device(): lax.all_gather(out_weight, 'seq', axis=1, tiled=True)  83.1 us
    dot_general x15, matrix products, compose(): jnp.einsum('hjk,hkl->hjl', earlier[1], later[0], precision=HIGHEST_PRECIS...  31 us
    dynamic_slice x30, local copies, waits for them, and re-layouts, hop(): longer = join(total, jax.tree.map(lambda part: part[position], pieces))  19.3 us
  transfers between devices with their start and end apart: 4, of which 4 were waited for; matrix products, arithmetic and copies ran while one was open for 9% of the time, Pallas kernels for 0%

commit v1 on v0

--- a/solution.py
+++ b/solution.py
@@ -2,6 +2,7 @@
 import jax.numpy as jnp
 from jax import lax
 from jax.sharding import PartitionSpec as P
+from jax.lax import all_to_all, axis_size
 
 BLOCK = 64
 HIGHEST_PRECISION = lax.Precision.HIGHEST
@@ -136,7 +137,15 @@
     )
     partial_sums = jnp.dot(
         mixed_heads,
-        lax.all_gather(out_weight, "seq", axis=1, tiled=True),
+        jnp.concatenate(
+            all_to_all(
+                jnp.stack([out_weight for _ in range(axis_size("seq"))], axis=0),
+                axis_name="seq",
+                split_axis=0,
+                concat_axis=0,
+            ),
+            axis=1,
+        ),
         preferred_element_type=jnp.float32,
     )
     return lax.psum_scatter(

time: 593 us -> 662 us (1.12)
  waiting for transfers between devices: 318 us -> 371 us
  starting transfers between devices: 0.12 us -> 8.47 us
    all_gather x2, waiting for transfers between devices: 227 us -> 364 us  [carried_in(): pieces = jax.tree.map(lambda part: lax.all_gather(part, axis), value)]
    all_gather x1 -> x0, waiting for transfers between devices: 83.1 us -> none  [per_device(): lax.all_gather(out_weight, 'seq', axis=1, tiled=True)]
    all_to_all x0 -> x1, starting transfers between devices: none -> 8.39 us  [per_device(): all_to_all(jnp.stack([out_weight for _ in range(axis_size('seq'))], axis=...]
  transfers between devices with their start and end apart: 4 -> 4, of which waited for: 4 -> 3; matrix products, arithmetic and copies ran while one was open for 9% -> 9% of each run, Pallas kernels for 0% -> 0%
where the time goes in v1:
time: 662 us; the launch traced here: 660 us
  waiting for transfers between devices  371 us (56%)
  other arithmetic  164 us (25%)
  matrix products  65.6 us (10%)
  local copies, waits for them, and re-layouts  32.1 us (5%)
  between operations  13.3 us (2%)
  starting transfers between devices  8.47 us (1%)
    all_gather x2, waiting for transfers between devices, carried_in(): pieces = jax.tree.map(lambda part: lax.all_gather(part, axis), value)  364 us
    another operation x8, other arithmetic, solve_block(): jax.scipy.linalg.solve_triangular(system, beta_heads[:, :, None] * right_...  159 us
    dot_general x15, matrix products, compose(): jnp.einsum('hjk,hkl->hjl', earlier[1], later[0], precision=HIGHEST_PRECIS...  30.9 us
    dynamic_slice x30, local copies, waits for them, and re-layouts, hop(): longer = join(total, jax.tree.map(lambda part: part[position], pieces))  19.2 us
  transfers between devices with their start and end apart: 4, of which 3 were waited for; matrix products, arithmetic and copies ran while one was open for 9% of the time, Pallas kernels for 0%

profile of v1, /device:TPU:0, one launch (start us, length us, event | category | flops | bytes accessed | tf_op | source)
XLA Modules:
  0.0 660.3 jit_solution(17176737119712990820)
XLA Ops:
  6.7 200.9 %while.31 = (s32[]{:T(128)}, f32[8,128,128]{2,1,0:T(8,128)S(1)}, f32[8,128,128]{1,2,0:T(8,128)S(1)}, f32[2,8,64,128]{3,2,0,1:T(8,128)}, f32[2,8,64,128]{3,2,0,1:...) while((s32[]{:T(128)}, f32[8,128,128]{2,1,0:T(8,128)S(1)}, ...), condition=%wide.region_3.4_spmd.clone, body=%wide.region_0.3_spmd.clone.sunk | while | flops 1915912320 | bytes 28152272 | solution.py:126
  13.8 79.2 %custom-call.10 = f32[8,1,128,128]{2,3,1,0:T(8,128)} custom-call(f32[8,1,128,128]{3,2,1,0:T(8,128)S(1)} %fusion.128), custom_call_target="InvertDiagBlocksLowerTriangular" | custom-call | tf_op jit(solution)/shard_map/while/body/eval_jaxpr/jit(_solve_triangular)/vmap()/triangular_solve | solution.py:61
  93.6 2.3 fusion.129
  114.1 79.2 %custom-call.10 = f32[8,1,128,128]{2,3,1,0:T(8,128)} custom-call(f32[8,1,128,128]{3,2,1,0:T(8,128)S(1)} %fusion.128), custom_call_target="InvertDiagBlocksLowerTriangular" | custom-call | tf_op jit(solution)/shard_map/while/body/eval_jaxpr/jit(_solve_triangular)/vmap()/triangular_solve | solution.py:61
  193.9 2.3 fusion.129
  210.8 4.3 stack.2
  215.1 8.4 %all-to-all-start = ((bf16[16,1024,256]{1,2,0:T(8,128)(2,1)}), bf16[16,1024,256]{1,2,0:T(8,128)(2,1)}, u32[]{:S(2)}, u32[]{:S(2)}) async-start(bf16[16,1024,256]{1,2,0:T(8,128)(2,1)} %stack.2), calls=%async_computation | async-start | bytes 16777216 | tf_op jit(solution)/shard_map/all_to_all | solution.py:141
  223.5 242.1 %all-gather.5.cloned.1.call-done = f32[128,128,128]{2,1,0:T(8,128)} async-done(((f32[8,128,128]{2,1,0:T(8,128)}), f32[128,128,128]{2,1,0:T(8,128)}) %all-gather.5.cloned.1.call-update) | async-done | bytes 8388624 | tf_op jit(solution)/shard_map/all_gather | solution.py:13
  465.6 121.8 %all-gather.7.cloned.1.call-done = f32[128,128,128]{2,1,0:T(8,128)} async-done(((f32[8,128,128]{2,1,0:T(8,128)}), f32[128,128,128]{2,1,0:T(8,128)}) %all-gather.7.cloned.1.call-update) | async-done | bytes 8388624 | tf_op jit(solution)/shard_map/all_gather | solution.py:13
  587.4 51.4 %while.32 = (s32[]{:T(128)}, f32[8,128,128]{1,2,0:T(8,128)S(1)}, s32[]{:T(128)}, f32[16,8,128,128]{3,2,1,0:T(8,128)}, f32[16,8,128,128]{3,2,1,0:T(8,128)}, /*index=5*/s32[]{:T(128)}, s32[]{:T(128)}) while((s32[]{:T(128)}, f32[8,128,128]{1,2,0:T(8,128)S(1)}, s32[]{:T(128)}, f32[16,8,128,128]{3,2,1,0:T(8,128)}, ...), condition=%wide.region_5.6_spmd.clone, body=%wide.region_4.5_spmd.clone.sunk | while | flops 201850880 | bytes 5769315 | solution.py:22
  588.9 2.1 fusion.136
  592.3 2.1 fusion.136
  595.7 2.1 fusion.136
  599.1 2.1 fusion.136
  602.5 2.1 fusion.136
  606.0 2.1 fusion.136
  609.4 2.1 fusion.136
  612.8 2.1 fusion.136
  619.6 2.1 fusion.136
  623.1 2.1 fusion.136
  626.5 2.1 fusion.136
  629.9 2.1 fusion.136
  639.7 7.3 %convolution_convert_fusion = bf16[128,4096]{1,0:T(8,128)(2,1)} fusion(bf16[1024,4096]{0,1:T(8,128)(2,1)} %bitcast.6, bf16[16,8,8,128]{3,2,1,0:T(8,128)(2,1)S(1)} %bitcast.211), kind=kOutput, calls=%fused_computation.74 | convolution fusion | flops 1074266112 | bytes 9699328 | tf_op jit(solution)/shard_map/dot_general | solution.py:138
  647.0 6.7 %reduce-scatter.2.cloned.1.call-done = bf16[128,2048]{1,0:T(8,128)(2,1)} async-done(((bf16[128,4096]{1,0:T(8,128)(2,1)}), bf16[128,2048]{1,0:T(8,128)(2,1)}) %reduce-scatter.2.cloned.1.call-update) | async-done | bytes 524304 | tf_op jit(solution)/shard_map/reduce_scatter | solution.py:151
  (140 shorter events, 63.5 us)
Async XLA Ops:
  6.5 459.1 %all-gather.5.cloned.1.call-start = ((), (), s32[]{:S(2)}) async-start(), calls=%async_computation.3 | async-start | bytes 8912896 | tf_op jit(solution)/shard_map/all_gather | solution.py:13
  207.7 1.1 copy-start
  208.8 378.7 %all-gather.7.cloned.1.call-start = ((), (), s32[]{:S(2)}) async-start(), calls=%async_computation.4 | async-start | bytes 8912896 | tf_op jit(solution)/shard_map/all_gather | solution.py:13
  215.1 424.6 %all-to-all-start = ((bf16[16,1024,256]{1,2,0:T(8,128)(2,1)}), bf16[16,1024,256]{1,2,0:T(8,128)(2,1)}, u32[]{:S(2)}, u32[]{:S(2)}) async-start(bf16[16,1024,256]{1,2,0:T(8,128)(2,1)} %stack.2), calls=%async_computation | async-start | bytes 16777216 | tf_op jit(solution)/shard_map/all_to_all | solution.py:141
  223.5 430.3 %reduce-scatter.2.cloned.1.call-start = ((), (), s32[]{:S(2)}) async-start(), calls=%async_computation.2 | async-start | bytes 1572864 | tf_op jit(solution)/shard_map/reduce_scatter | solution.py:151
  587.4 51.4 %copy-start.1 = (f32[2,8,64,128]{3,2,0,1:T(8,128)S(1)}, f32[2,8,64,128]{3,2,0,1:T(8,128)}, u32[]{:S(2)}) copy-start(f32[2,8,64,128]{3,2,0,1:T(8,128)} %get-tuple-element.164) | copy-start | bytes 1572868
  587.4 51.4 %copy-start.2 = (f32[2,8,64,128]{3,2,0,1:T(8,128)S(1)}, f32[2,8,64,128]{3,2,0,1:T(8,128)}, u32[]{:S(2)}) copy-start(f32[2,8,64,128]{3,2,0,1:T(8,128)} %get-tuple-element.168) | copy-start | bytes 1572868
Sparse Core Ops, SparseCore 0:
  208.9 256.6 all-gather.4
  468.4 119.0 all-gather.6
  647.2 6.5 reduce-scatter.1
